TPU v7x, 32 devices: a whole 2x2x4 slice. The times are simulated.
32 devices in a mesh: dp: 16 (over z, y, x), member: 2 (over core).
Axes of the slice: x: 2, y: 2, z: 4, core: 2. Of those that a mesh axis runs over, the one named last changes fastest.
Arguments:
- inputs: bfloat16 [24576, 393], P(('dp', 'member')), may hold values from -256 to 256
- targets: bfloat16 [24576, 377], P(('dp', 'member')), may hold values from -6 to 6
- bootstrap: int32 [2, 24576], P('member', 'dp'), may hold values from 0 to 1535
- lower_weight: bfloat16 [2, 393, 1024], P('member'), may hold values from -0.3125 to 0.3125
- lower_shift: float32 [2, 1024], P('member'), may hold values from -3 to 3
- upper_weight: bfloat16 [2, 1024, 377], P('member'), may hold values from -0.1875 to 0.1875
- upper_shift: float32 [2, 377], P('member'), may hold values from -3 to 3
- log_var: float32 [2, 377], P('member'), may hold values from -1 to 1
Outputs:
- lower_grad: float32 [2, 1024, 393], P('member', 'dp')
- bias_grad: float32 [2, 1024], P('member', 'dp')
- upper_grad: float32 [2, 1024, 377], P('member', 'dp')
- offset_grad: float32 [2, 377], P('member')
- noise_grad: float32 [2, 377], P('member')
- member_loss: float32 [2], P('member')
Inputs may be any that keep to these rules, and one draw needn't show every extreme that they name: bootstrap[m, r] is an offset within the aligned block of 1536 rows that holds row r.
All inputs are finite; a program needn't handle non-finite values.
Results may differ from a plain program's by a relative error of at most 0.00076.
Values may be sent and summed in bfloat16 or wider, within the bound.
A program may use at most 64 MiB of HBM per device.

v0:
```python
import jax
import jax.numpy as jnp
from jax import lax
from jax.sharding import PartitionSpec as P

H = 1024


def member_pass(
    picked, goal_rows, lower_weight, lower_shift, upper_weight, upper_shift, log_var, row_count
):
    pre_act = jnp.dot(picked, lower_weight, preferred_element_type=jnp.float32) + lower_shift
    hidden = jax.nn.silu(pre_act).astype(jnp.bfloat16)
    pred_mean = jnp.dot(hidden, upper_weight, preferred_element_type=jnp.float32) + upper_shift
    residual = pred_mean - goal_rows.astype(jnp.float32)
    scaled_err = residual * jnp.exp(-log_var)
    member_loss = 0.5 * jnp.sum(residual * scaled_err + log_var) / row_count
    grad_mean = scaled_err / row_count
    offset_grad = jnp.sum(grad_mean, axis=0)
    noise_grad = 0.5 * jnp.sum(1.0 - residual * scaled_err, axis=0) / row_count
    grad_half = grad_mean.astype(jnp.bfloat16)
    grad_hidden = lax.dot_general(
        grad_half, upper_weight, (((1,), (1,)), ((), ())), preferred_element_type=jnp.float32
    )
    gate_sig = jax.nn.sigmoid(pre_act)
    grad_pre = grad_hidden * gate_sig * (1.0 + pre_act * (1.0 - gate_sig))
    bias_grad = jnp.sum(grad_pre, axis=0)
    pre_half = grad_pre.astype(jnp.bfloat16)
    return (hidden, grad_half, pre_half, bias_grad, offset_grad, noise_grad, member_loss)


def outer_rows(left, right):
    return lax.dot_general(
        left, right, (((0,), (0,)), ((), ())), preferred_element_type=jnp.float32
    )


def feature_stats(inputs):
    values = inputs.astype(jnp.float32)
    row_count = inputs.shape[0] * lax.axis_size("dp") * lax.axis_size("member")
    col_total = lax.psum(jnp.sum(values, axis=0), ("dp", "member"))
    feature_mean = col_total / row_count
    centered = values - feature_mean
    col_spread = lax.psum(jnp.sum(centered * centered, axis=0), ("dp", "member"))
    feature_var = col_spread / row_count
    return (feature_mean, 1.0 / jnp.sqrt(feature_var + 1e-06))


def per_device(
    inputs, targets, bootstrap, lower_weight, lower_shift, upper_weight, upper_shift, log_var
):
    feature_mean, feature_scale = feature_stats(inputs)
    own_rows = ((inputs.astype(jnp.float32) - feature_mean) * feature_scale).astype(jnp.bfloat16)
    row_block, goal_block = (
        lax.all_gather(own_rows, "member", axis=0, tiled=True),
        lax.all_gather(targets, "member", axis=0, tiled=True),
    )
    row_count = goal_block.shape[0]
    pick_row = bootstrap[0]
    picked = row_block[pick_row]
    passes = [
        (picked,)
        + member_pass(
            picked,
            goal_block[pick_row],
            lower_weight[0],
            lower_shift[0],
            upper_weight[0],
            upper_shift[0],
            log_var[0],
            row_count,
        )
    ]
    share = H // lax.axis_size("dp")
    lower_list, upper_list = ([], [])
    picked, hidden, grad_half, pre_half, bias_one, offset_one, noise_one, loss_one = passes[0]

    def upper_term(start, count, hidden=hidden, grad_half=grad_half):
        return outer_rows(hidden, grad_half)

    def lower_term(start, count, pre_half=pre_half, picked=picked):
        return outer_rows(pre_half, picked)

    upper_list.append(
        lax.psum_scatter(
            upper_term(jnp.int32(0), share * lax.axis_size("dp")),
            "dp",
            scatter_dimension=0,
            tiled=True,
        )
    )
    lower_list.append(
        lax.psum_scatter(
            lower_term(jnp.int32(0), share * lax.axis_size("dp")),
            "dp",
            scatter_dimension=0,
            tiled=True,
        )
    )
    lower_grad = jnp.stack(lower_list)
    upper_grad = jnp.stack(upper_list)
    bias_sum = jnp.stack([item[4] for item in passes])
    offset_sum = jnp.stack([item[5] for item in passes])
    noise_sum = jnp.stack([item[6] for item in passes])
    loss_sum = jnp.stack([item[7] for item in passes])
    bias_total, offset_grad, noise_grad, member_loss = lax.psum(
        (bias_sum, offset_sum, noise_sum, loss_sum), "dp"
    )
    bias_grad = lax.dynamic_slice_in_dim(bias_total, lax.axis_index("dp") * share, share, 1)
    return (lower_grad, bias_grad, upper_grad, offset_grad, noise_grad, member_loss)


def solution(mesh):
    return jax.shard_map(
        per_device,
        mesh=mesh,
        in_specs=(
            P(("dp", "member"), None),
            P(("dp", "member"), None),
            P("member", "dp"),
            P("member", None, None),
            P("member", None),
            P("member", None, None),
            P("member", None),
            P("member", None),
        ),
        out_specs=(
            P("member", "dp", None),
            P("member", "dp"),
            P("member", "dp", None),
            P("member", None),
            P("member", None),
            P("member"),
        ),
        check_vma=False,
    )
```

profile of v0, /device:TPU:0, one launch (start us, length us, event | category | flops | bytes accessed | tf_op | source)
XLA Modules:
  0.0 339.9 jit_solution(8934908891919403699)
XLA Ops:
  7.2 0.0 copy-start
  7.2 0.0 all-gather.5.cloned.1.call-start
  7.2 0.7 all-gather.5.cloned.1.call-update
  7.9 0.0 copy-start.3
  7.9 0.0 copy-start.2
  7.9 0.0 copy-start.4
  7.9 0.0 all-gather.3.cloned.1.call-start
  8.0 1.3 copy.15
  9.3 0.2 convert_reduce_fusion
  9.5 42.0 %psum.42 = f32[393]{0:T(512)S(1)} all-reduce(f32[393]{0:T(512)S(1)} %convert_reduce_fusion), channel_id=1, replica_groups=mesh['dp'=16,'member'=2] {'dp','member'}, use_global_device_ids=true, to_apply=%region_1.0 | all-reduce | flops 393 | bytes 3144 | tf_op jit(solution)/shard_map/psum | solution.py:41
  51.5 0.3 fusion.7
  51.8 40.1 %psum.43 = f32[393]{0:T(512)S(1)} all-reduce(f32[393]{0:T(512)S(1)} %fusion.7), channel_id=1, replica_groups=mesh['dp'=16,'member'=2] {'dp','member'}, use_global_device_ids=true, to_apply=%region_3.0 | all-reduce | flops 393 | bytes 3144 | tf_op jit(solution)/shard_map/psum | solution.py:44
  91.9 1.1 fusion.8
  93.0 0.0 all-gather.3.cloned.1.call-update
  93.0 0.0 reduce-scatter.5.cloned.1.call-start
  93.1 0.0 copy-done.3
  93.1 0.0 copy-done.2
  93.2 0.0 copy-done.4
  93.2 0.0 all-gather.5.cloned.1.call-done
  93.2 6.4 %gather_fusion.1 = bf16[1536,377]{1,0:T(8,128)(2,1)} fusion(bf16[1536,377]{1,0:T(8,128)(2,1)} %all-gather.5.cloned.1.call-done, s32[2048]{0:T(1024)S(1)} %pad_clamp_fusion), kind=kCustom, calls=%fused_computation.1 | custom fusion | bytes 2322432 | tf_op jit(solution)/shard_map/gather | solution.py:65
  99.7 0.0 copy-start.6
  99.7 3.9 %all-gather.3.cloned.1.call-done = bf16[1536,393]{1,0:T(8,128)(2,1)} async-done(((bf16[768,393]{1,0:T(8,128)(2,1)}), bf16[1536,393]{1,0:T(8,128)(2,1)}) %all-gather.3.cloned.1.call-update) | async-done | bytes 1207312 | tf_op jit(solution)/shard_map/all_gather | solution.py:55
  103.6 6.5 %gather_fusion = bf16[1536,393]{1,0:T(8,128)(2,1)S(1)} fusion(bf16[1536,393]{1,0:T(8,128)(2,1)} %all-gather.3.cloned.1.call-done, s32[2048]{0:T(1024)S(1)} %pad_clamp_fusion), kind=kCustom, calls=%fused_computation | custom fusion | bytes 2420736 | tf_op jit(solution)/shard_map/gather | solution.py:60
  110.1 0.0 copy-done
  110.1 0.0 copy-done.6
  110.1 0.0 copy-start.1
  110.1 0.0 copy-start.5
  110.1 5.1 %multiply_convert_fusion = (bf16[1536,1024]{1,0:T(8,128)(2,1)S(1)}, f32[1536,1024]{1,0:T(8,128)}) fusion(f32[1024]{0:T(1024)S(1)} %bitcast.29, bf16[1536,393]{1,0:T(8,128)(2,1)S(1)} %gather_fusion, bf16[1,393,1024]{2,1,0:T(8,128)(2,1)S(1)} %copy-done), kind=kOutput, calls=%fused_computation.3 | convolution fusion | flops 1245708288 | bytes 11453440 | tf_op jit(solution)/shard_map/dot_general | solution.py:12
  115.2 0.0 copy-done.1
  115.2 0.0 copy-done.5
  115.2 3.2 add_reduce_fusion
  118.4 0.0 copy-start.7
  118.4 1.4 copy-done.7
  119.8 3.0 fusion.13
  122.8 0.0 reduce-scatter.5.cloned.1.call-update
  122.9 0.2 reduce-scatter.3.cloned.1.call-start
  123.1 6.4 %fusion.20 = (f32[1024]{0:T(1024)S(1)}, bf16[1536,1024]{1,0:T(8,128)(2,1)S(1)}) fusion(f32[1536,1024]{1,0:T(8,128)} %get-tuple-element.16, f32[1024]{0:T(1024)S(1)} %bitcast.30, bf16[1,1024,377]{2,1,0:T(8,128)(2,1)S(1)} %copy-done.5, f32[1536,377]{1,0:T(8,128)} %copy-done.7, f32[377]{0:T(512)S(1)} %get-tuple-element.10), kind=kOutput, calls=%fused_computation.37 | convolution fusion | flops 1204977152 | bytes 12535268 | tf_op jit(solution)/shard_map/dot_general | solution.py:22
  129.5 3.2 fusion
  132.7 0.0 reduce-scatter.3.cloned.1.call-update
  133.4 43.6 %all-reduce = (f32[1,1024]{1,0:T(1,128)S(1)}, f32[1,377]{1,0:T(1,128)}, f32[1,377]{1,0:T(1,128)}, f32[1]{0:T(128)}) all-reduce(f32[1,1024]{1,0:T(1,128)S(1)} %bitcast.26, f32[1,377]{1,0:T(1,128)S(1)} %stack.19, f32[1,377]{1,0:T(1,128)S(1)} %div.37, f32[1]{0:T(128)} %bitcast.7), channel_id=1, replica_groups=mesh['dp'=16,'member'=2] {'dp'}, use_global_device_ids=true, to_apply=%region_6.7 | all-reduce | flops 1779 | bytes 14232 | tf_op jit(solution)/shard_map/psum | solution.py:106
  177.0 0.6 constant_dynamic-slice_fusion
  177.6 72.6 %reduce-scatter.5.cloned.1.call-done = f32[64,377]{1,0:T(8,128)} async-done(((f32[1024,377]{1,0:T(8,128)}), f32[64,377]{1,0:T(8,128)}) %reduce-scatter.5.cloned.1.call-update) | async-done | bytes 96528 | tf_op jit(solution)/shard_map/reduce_scatter | solution.py:85
  250.3 83.1 %reduce-scatter.3.cloned.1.call-done = f32[64,393]{1,0:T(8,128)} async-done(((f32[1024,393]{1,0:T(8,128)}), f32[64,393]{1,0:T(8,128)}) %reduce-scatter.3.cloned.1.call-update) | async-done | bytes 100624 | tf_op jit(solution)/shard_map/reduce_scatter | solution.py:93
  (9 shorter events, 0.1 us)
Async XLA Ops:
  7.2 102.9 %copy-start = (bf16[1,393,1024]{2,1,0:T(8,128)(2,1)S(1)}, bf16[1,393,1024]{2,1,0:T(8,128)(2,1)}, u32[]{:S(2)}) copy-start(bf16[1,393,1024]{2,1,0:T(8,128)(2,1)} %param.11) | copy-start | bytes 2414596
  7.2 86.0 %all-gather.5.cloned.1.call-start = ((), (), s32[]{:S(2)}) async-start(), calls=%async_computation.3 | async-start | bytes 1769472 | tf_op jit(solution)/shard_map/all_gather | solution.py:56
  7.9 85.2 %copy-start.3 = (f32[1,377]{1,0:T(1,128)S(1)}, f32[1,377]{1,0:T(1,128)}, u32[]{:S(2)}) copy-start(f32[1,377]{1,0:T(1,128)} %param.14) | copy-start | bytes 4528
  7.9 85.2 %copy-start.2 = (s32[1,1536]{1,0:T(1,128)S(1)}, s32[1,1536]{1,0:T(1,128)}, u32[]{:S(2)}) copy-start(s32[1,1536]{1,0:T(1,128)} %param.10) | copy-start | bytes 18436
  7.9 85.2 %copy-start.4 = (f32[1,377]{1,0:T(1,128)S(1)}, f32[1,377]{1,0:T(1,128)}, u32[]{:S(2)}) copy-start(f32[1,377]{1,0:T(1,128)} %param.15) | copy-start | bytes 4528
  7.9 95.6 %all-gather.3.cloned.1.call-start = ((), (), s32[]{:S(2)}) async-start(), calls=%async_computation.2 | async-start | bytes 2359296 | tf_op jit(solution)/shard_map/all_gather | solution.py:55
  93.0 157.2 %reduce-scatter.5.cloned.1.call-start = ((), (), s32[]{:S(2)}) async-start(), calls=%async_computation.5 | async-start | bytes 1671168 | tf_op jit(solution)/shard_map/reduce_scatter | solution.py:85
  99.7 10.4 %copy-start.6 = (f32[1,1024]{1,0:T(1,128)S(1)}, f32[1,1024]{1,0:T(1,128)}, u32[]{:S(2)}) copy-start(f32[1,1024]{1,0:T(1,128)} %param.12) | copy-start | bytes 12292
  110.1 5.1 %copy-start.1 = (bf16[1536,377]{1,0:T(8,128)(2,1)S(1)}, bf16[1536,377]{1,0:T(8,128)(2,1)}, u32[]{:S(2)}) copy-start(bf16[1536,377]{1,0:T(8,128)(2,1)} %gather_fusion.1) | copy-start | bytes 3474436
  110.1 5.1 %copy-start.5 = (bf16[1,1024,377]{2,1,0:T(8,128)(2,1)S(1)}, bf16[1,1024,377]{2,1,0:T(8,128)(2,1)}, u32[]{:S(2)}) copy-start(bf16[1,1024,377]{2,1,0:T(8,128)(2,1)} %param.13) | copy-start | bytes 2316292
  118.4 1.4 copy-start.7
  122.9 210.5 %reduce-scatter.3.cloned.1.call-start = ((), (), s32[]{:S(2)}) async-start(), calls=%async_computation.4 | async-start | bytes 2228224 | tf_op jit(solution)/shard_map/reduce_scatter | solution.py:93
Sparse Core Ops, SparseCore 0:
  9.5 11.9 all-gather.4
  93.1 10.3 all-gather.2
  123.0 127.2 reduce-scatter.4
  253.0 80.3 reduce-scatter.2
where the time goes:
time: 340 us
  waiting for transfers between devices  160 us (47%)
  blocking collectives  126 us (37%)
  matrix products  20.9 us (6%)
  local copies, waits for them, and re-layouts  16.3 us (5%)
  between operations  14.6 us (4%)
    reduce_scatter x1, waiting for transfers between devices, per_device(): lax.psum_scatter(lower_term(jnp.int32(0), share * lax.axis_size('dp')), '...  83.1 us
    reduce_scatter x1, waiting for transfers between devices, per_device(): lax.psum_scatter(upper_term(jnp.int32(0), share * lax.axis_size('dp')), '...  72.6 us
    psum x1, blocking collectives, per_device(): lax.psum((bias_sum, offset_sum, noise_sum, loss_sum), 'dp')  43.6 us
    psum x1, blocking collectives, feature_stats(): col_total = lax.psum(jnp.sum(values, axis=0), ('dp', 'member'))  42 us
    psum x1, blocking collectives, feature_stats(): lax.psum(jnp.sum(centered * centered, axis=0), ('dp', 'member'))  40.1 us
  transfers between devices with their start and end apart: 4, of which 3 were waited for; matrix products, arithmetic and copies ran while one was open for 6% of the time, Pallas kernels for 0%

commit v1 on v0

v1 whole, which is shorter than its diff:
```python
import functools

import jax
import jax.numpy as jnp
from jax import lax
from jax.experimental import pallas as pl
from jax.experimental.pallas import tpu as pltpu
from jax.sharding import PartitionSpec as P

MESH = pl.DeviceIdType.MESH
LANES = 128
VMEM_LIMIT = 60 * 1024 * 1024


def pad_lanes(width):
    return -(-width // LANES) * LANES


def merge_stats(slots, count, width, each):
    total = jnp.zeros((1, width), jnp.float32)
    for i in range(count):
        total = total + slots[i, 0:1, 0:width]
    mean = total / (count * each)
    spread = jnp.zeros((1, width), jnp.float32)
    for i in range(count):
        gap = slots[i, 0:1, 0:width] / each - mean
        spread = spread + (slots[i, 1:2, 0:width] + each * (gap * gap))
    return total, spread


def rows_kernel(
    n, m, x_ref, t_ref, rows_ref, goals_ref,
    member_slots, dp_slots, member_sems, dp_sems, rows_sems, goal_sems,
):
    d, c = lax.axis_index("dp"), lax.axis_index("member")
    count, width = x_ref.shape
    barrier = pltpu.get_barrier_semaphore()
    for o in range(1, m):
        pl.semaphore_signal(barrier, 1, device_id=(d, lax.rem(c + o, m)), device_id_type=MESH)
    for o in range(1, n):
        pl.semaphore_signal(barrier, 1, device_id=(lax.rem(d + o, n), c), device_id_type=MESH)

    member_slots[c] = jnp.zeros(member_slots.shape[1:], jnp.float32)
    dp_slots[d] = jnp.zeros(dp_slots.shape[1:], jnp.float32)
    values = x_ref[...].astype(jnp.float32)
    total = jnp.sum(values, axis=0, keepdims=True)
    gap = values - total / count
    member_slots[c, 0:1, 0:width] = total
    member_slots[c, 1:2, 0:width] = jnp.sum(gap * gap, axis=0, keepdims=True)
    pl.semaphore_wait(barrier, m - 1 + n - 1)

    def to_member(src, dst, sems, o):
        return pltpu.make_async_remote_copy(
            src_ref=src, dst_ref=dst, send_sem=sems.at[0, o], recv_sem=sems.at[1, o],
            device_id=(d, lax.rem(c + o, m)), device_id_type=MESH,
        )

    stat_copies = [
        to_member(member_slots.at[c], member_slots.at[c], member_sems, o) for o in range(1, m)
    ]
    for copy in stat_copies:
        copy.start()
    goal_copies = [to_member(t_ref, goals_ref.at[c], goal_sems, o) for o in range(1, m)]
    for copy in goal_copies:
        copy.start()
    for copy in stat_copies:
        copy.wait()
    total, spread = merge_stats(member_slots, m, width, count)
    dp_slots[d, 0:1, 0:width] = total
    dp_slots[d, 1:2, 0:width] = spread
    dp_copies = [
        pltpu.make_async_remote_copy(
            src_ref=dp_slots.at[d], dst_ref=dp_slots.at[d],
            send_sem=dp_sems.at[0, o], recv_sem=dp_sems.at[1, o],
            device_id=(lax.rem(d + o, n), c), device_id_type=MESH,
        )
        for o in range(1, n)
    ]
    for copy in dp_copies:
        copy.start()
    goals_ref[c] = t_ref[...]
    edge = width // LANES * LANES
    if rows_ref.shape[2] > width:
        rows_ref[c, :, edge:] = jnp.zeros((count, rows_ref.shape[2] - edge), rows_ref.dtype)
    for copy in dp_copies:
        copy.wait()
    total, spread = merge_stats(dp_slots, n, width, count * m)
    mean = total / (count * m * n)
    scale = 1.0 / jnp.sqrt(spread / (count * m * n) + 1e-06)
    rows_ref[c, :, 0:width] = ((x_ref[...].astype(jnp.float32) - mean) * scale).astype(jnp.bfloat16)
    row_copies = [to_member(rows_ref.at[c], rows_ref.at[c], rows_sems, o) for o in range(1, m)]
    for copy in row_copies:
        copy.start()
    for copy in goal_copies + row_copies:
        copy.wait()


def shared_rows(n, m, inputs, targets):
    count, width = inputs.shape
    goal_width = targets.shape[1]
    wide = pad_lanes(width)
    rows, goals = pl.pallas_call(
        functools.partial(rows_kernel, n, m),
        out_shape=(
            jax.ShapeDtypeStruct((m, count, wide), jnp.bfloat16),
            jax.ShapeDtypeStruct((m, count, goal_width), targets.dtype),
        ),
        in_specs=[pl.BlockSpec(memory_space=pltpu.VMEM)] * 2,
        out_specs=(pl.BlockSpec(memory_space=pltpu.VMEM),) * 2,
        scratch_shapes=[
            pltpu.VMEM((m, 8, wide), jnp.float32),
            pltpu.VMEM((n, 8, wide), jnp.float32),
            pltpu.SemaphoreType.DMA((2, m)),
            pltpu.SemaphoreType.DMA((2, n)),
            pltpu.SemaphoreType.DMA((2, m)),
            pltpu.SemaphoreType.DMA((2, m)),
        ],
        compiler_params=pltpu.CompilerParams(
            collective_id=1, has_side_effects=True, vmem_limit_bytes=VMEM_LIMIT
        ),
        name="share_rows",
    )(inputs, targets)
    return rows.reshape(m * count, wide), goals.reshape(m * count, goal_width)


def bit_orders(bits):
    forward = list(range(bits))
    swapped = [1, 0] + forward[2:] if bits > 1 else forward
    late = forward[2:] + forward[:2]
    return forward, swapped, late


def grads_kernel(n, bits, plan, l_ref, u_ref, s_ref, lo_ref, uo_ref, so_ref, small, *rest):
    groups = len(plan)
    slots = [rest[g * bits:(g + 1) * bits] for g in range(groups)]
    sems, small_sems = rest[groups * bits], rest[groups * bits + 1]
    d, c = lax.axis_index("dp"), lax.axis_index("member")
    mine = [lax.rem(d // 2 ** b, 2) for b in range(bits)]
    peer = [d + (1 - 2 * mine[b]) * 2 ** b for b in range(bits)]
    barrier = pltpu.get_barrier_semaphore()
    for o in range(1, n):
        pl.semaphore_signal(barrier, 1, device_id=(lax.rem(d + o, n), c), device_id_type=MESH)
    pl.semaphore_wait(barrier, n - 1)

    def half(ref, left, bit, side, lanes):
        where = tuple(side if b == bit else slice(None) for b in left)
        return where + (slice(None), lanes)

    def begin(g, step):
        which, start, order = plan[g]
        left = [b for b in reversed(range(bits)) if b not in order[:step]]
        bit = order[step]
        if step == 0:
            ref, lanes = (l_ref, u_ref)[which], pl.ds(start, LANES)
        else:
            ref, lanes = slots[g][step - 1], slice(None)
        copy = pltpu.make_async_remote_copy(
            src_ref=ref.at[half(ref, left, bit, 1 - mine[bit], lanes)],
            dst_ref=slots[g][step],
            send_sem=sems.at[0, g, step], recv_sem=sems.at[1, g, step],
            device_id=(peer[bit], c), device_id_type=MESH,
        )
        copy.start()
        return copy, ref, half(ref, left, bit, mine[bit], lanes)

    flying = [begin(g, 0) for g in range(groups)]
    small[d] = s_ref[...]
    small_copies = [
        pltpu.make_async_remote_copy(
            src_ref=s_ref, dst_ref=small.at[d],
            send_sem=small_sems.at[0, o], recv_sem=small_sems.at[1, o],
            device_id=(lax.rem(d + o, n), c), device_id_type=MESH,
        )
        for o in range(1, n)
    ]
    for copy in small_copies:
        copy.start()
    sent = []
    for step in range(bits):
        for g in range(groups):
            copy, ref, own = flying[g]
            copy.wait_recv()
            sent.append(copy)
            landed = slots[g][step]
            summed = landed[...] + ref[own]
            if step < bits - 1:
                landed[...] = summed
                flying[g] = begin(g, step + 1)
            else:
                which, start, order = plan[g]
                (lo_ref, uo_ref)[which][:, start:start + LANES] = summed
    for copy in sent:
        copy.wait_send()
    for copy in small_copies:
        copy.wait()
    total = small[0]
    for i in range(1, n):
        total = total + small[i]
    so_ref[...] = total


def reduce_grads(n, lower, upper, small):
    bits = n.bit_length() - 1
    assert n == 2 ** bits
    share = lower.shape[0] // n
    parts = [(0, t) for t in range(0, lower.shape[1], LANES)]
    parts += [(1, t) for t in range(0, upper.shape[1], LANES)]
    forward, swapped, late = bit_orders(bits)
    pattern = [forward, swapped, late, forward, swapped, forward, swapped]
    plan = [part + (tuple(pattern[i % len(pattern)]),) for i, part in enumerate(parts)]
    tree = (2,) * bits
    slots = []
    for _ in plan:
        for step in range(bits):
            slots.append(pltpu.VMEM((2,) * (bits - 1 - step) + (share, LANES), jnp.float32))
    return pl.pallas_call(
        functools.partial(grads_kernel, n, bits, plan),
        out_shape=(
            jax.ShapeDtypeStruct((share, lower.shape[1]), jnp.float32),
            jax.ShapeDtypeStruct((share, upper.shape[1]), jnp.float32),
            jax.ShapeDtypeStruct(small.shape, jnp.float32),
        ),
        in_specs=[pl.BlockSpec(memory_space=pltpu.VMEM)] * 3,
        out_specs=(pl.BlockSpec(memory_space=pltpu.VMEM),) * 3,
        scratch_shapes=[pltpu.VMEM((n,) + small.shape, jnp.float32)]
        + slots
        + [
            pltpu.SemaphoreType.DMA((2, len(plan), bits)),
            pltpu.SemaphoreType.DMA((2, n)),
        ],
        compiler_params=pltpu.CompilerParams(
            collective_id=2, has_side_effects=True, vmem_limit_bytes=VMEM_LIMIT
        ),
        name="reduce_grads",
    )(
        lower.reshape(tree + (share, lower.shape[1])),
        upper.reshape(tree + (share, upper.shape[1])),
        small,
    )


def outer_rows(left, right):
    return lax.dot_general(
        left, right, (((0,), (0,)), ((), ())), preferred_element_type=jnp.float32
    )


def per_device(
    inputs, targets, bootstrap, lower_weight, lower_shift, upper_weight, upper_shift, log_var
):
    n, m = lax.axis_size("dp"), lax.axis_size("member")
    width, out = inputs.shape[1], targets.shape[1]
    wide, out_wide = pad_lanes(width + 1), pad_lanes(out)
    row_block, goal_block = shared_rows(n, m, inputs, targets)
    row_count = goal_block.shape[0]
    spot = lax.broadcasted_iota(jnp.int32, (row_count, row_count), 1)
    choose = (bootstrap[0][:, None] == spot).astype(jnp.bfloat16)
    picked = jnp.dot(choose, row_block, preferred_element_type=jnp.float32).astype(jnp.bfloat16)
    goal_rows = jnp.dot(choose, goal_block, preferred_element_type=jnp.float32)
    lower_weight, upper_weight = lower_weight[0], upper_weight[0]
    weight_wide = jnp.pad(lower_weight, ((0, picked.shape[1] - width), (0, 0)))
    pre_act = jnp.dot(picked, weight_wide, preferred_element_type=jnp.float32) + lower_shift[0]
    gate_sig = jax.nn.sigmoid(pre_act)
    hidden = (pre_act * gate_sig).astype(jnp.bfloat16)
    pred_mean = jnp.dot(hidden, upper_weight, preferred_element_type=jnp.float32) + upper_shift[0]
    residual = pred_mean - goal_rows
    scaled_err = residual * jnp.exp(-log_var[0])
    product = residual * scaled_err
    product_sum = jnp.sum(product, axis=0)
    member_loss = 0.5 * (jnp.sum(product_sum) + row_count * jnp.sum(log_var[0])) / row_count
    grad_mean = scaled_err / row_count
    offset_grad = jnp.sum(grad_mean, axis=0)
    noise_grad = 0.5 * jnp.sum(1.0 - product, axis=0) / row_count
    grad_half = grad_mean.astype(jnp.bfloat16)
    grad_hidden = lax.dot_general(
        grad_half, upper_weight, (((1,), (1,)), ((), ())), preferred_element_type=jnp.float32
    )
    grad_pre = grad_hidden * gate_sig * (1.0 + pre_act * (1.0 - gate_sig))
    bias = jnp.sum(grad_pre, axis=0)
    pre_half = grad_pre.astype(jnp.bfloat16)
    upper = outer_rows(hidden, jnp.pad(grad_half, ((0, 0), (0, out_wide - out))))
    lower = outer_rows(pre_half, picked)
    column = lax.broadcasted_iota(jnp.int32, lower.shape, 1)
    lower = jnp.where(column == width, bias[:, None], lower)
    small = jnp.pad(
        jnp.stack([offset_grad, noise_grad, jnp.full((out,), member_loss)]),
        ((0, 5), (0, out_wide - out)),
    )
    lower, upper, small = reduce_grads(n, lower, upper, small)
    return (
        lower[None, :, :width],
        lower[None, :, width],
        upper[None, :, :out],
        small[0:1, :out],
        small[1:2, :out],
        small[2, 0:1],
    )


def solution(mesh):
    return jax.shard_map(
        per_device,
        mesh=mesh,
        in_specs=(
            P(("dp", "member"), None),
            P(("dp", "member"), None),
            P("member", "dp"),
            P("member", None, None),
            P("member", None),
            P("member", None, None),
            P("member", None),
            P("member", None),
        ),
        out_specs=(
            P("member", "dp", None),
            P("member", "dp"),
            P("member", "dp", None),
            P("member", None),
            P("member", None),
            P("member"),
        ),
        check_vma=False,
    )
```

time: 340 us -> 107 us (0.31)
  waiting for transfers between devices: 160 us -> 0 us
  blocking collectives: 126 us -> 0 us
  Pallas kernels: 0 us -> 66.3 us
  between operations: 14.6 us -> 2.11 us
  matrix products: 20.9 us -> 27.6 us
  local copies, waits for them, and re-layouts: 16.3 us -> 10.2 us
    reduce_scatter x2 -> x0, waiting for transfers between devices: 156 us -> none  [the longest x1 83.1 us: per_device(): lax.psum_scatter(lower_term(jnp.int32(0), share * lax.axis_size('dp')), '...]
    psum x3 -> x0, blocking collectives: 126 us -> none  [the longest x1 43.6 us: per_device(): lax.psum((bias_sum, offset_sum, noise_sum, loss_sum), 'dp')]
    pallas_call x0 -> x2, Pallas kernels: none -> 66.3 us  [the longest x1 48.2 us: reduce_grads(): pl.pallas_call(functools.partial(grads_kernel, n, bits, plan), out_shape=...]
    gather x2 -> x0, local copies, waits for them, and re-layouts: 12.9 us -> none  [the longest x1 6.47 us: per_device(): picked = row_block[pick_row]]
    dot_general x3 -> x5, matrix products: 14.7 us -> 21.4 us  [the longest x1 5.22 us: per_device(): jnp.dot(picked, weight_wide, preferred_element_type=jnp.float32)]
    slice x0 -> x3, local copies, waits for them, and re-layouts: none -> 4 us  [the longest x1 1.46 us: per_device(): lower[None, :, width]]
    all_gather x2 -> x0, waiting for transfers between devices: 3.93 us -> none  [the longest x1 3.91 us: per_device(): lax.all_gather(own_rows, 'member', axis=0, tiled=True)]
  transfers between devices with their start and end apart: 4 -> 0, of which waited for: 3 -> 0; matrix products, arithmetic and copies ran while one was open for 6% -> 0% of each run, Pallas kernels for 0% -> 0%
where the time goes in v1:
time: 107 us
  Pallas kernels  66.3 us (62%)
  matrix products  27.6 us (26%)
  local copies, waits for them, and re-layouts  10.2 us (10%)
  between operations  2.11 us (2%)
    pallas_call x1, Pallas kernels, reduce_grads(): pl.pallas_call(functools.partial(grads_kernel, n, bits, plan), out_shape=...  48.2 us
    pallas_call x1, Pallas kernels, shared_rows(): pl.pallas_call(functools.partial(rows_kernel, n, m), out_shape=(jax.Shape...  18.1 us
    dot_general x2, matrix products, outer_rows(): lax.dot_general(left, right, (((0,), (0,)), ((), ())), preferred_element_...  6.19 us
    dot_general x1, matrix products, per_device(): jnp.dot(picked, weight_wide, preferred_element_type=jnp.float32)  5.22 us
    dot_general x1, matrix products, per_device(): jnp.dot(choose, row_block, preferred_element_type=jnp.float32)  4.22 us
    dot_general x1, matrix products, per_device(): goal_rows = jnp.dot(choose, goal_block, preferred_element_type=jnp.float32)  4.21 us
    dot_general x1, matrix products, per_device(): lax.dot_general(grad_half, upper_weight, (((1,), (1,)), ((), ())), prefer...  3.9 us
    dot_general x1, matrix products, per_device(): jnp.dot(hidden, upper_weight, preferred_element_type=jnp.float32)  3.87 us

profile of v1, /device:TPU:0, one launch (start us, length us, event | category | flops | bytes accessed | tf_op | source)
XLA Modules:
  0.0 106.9 jit_solution(8056267715008385666)
XLA Ops:
  0.6 0.0 copy-start
  0.6 0.0 copy-start.1
  0.7 2.3 %copy.15.x_ref = bf16[768,393]{1,0:T(8,128)(2,1)} copy(bf16[768,393]{0,1:T(8,128)(2,1)} %param.8) | data formatting | bytes 1207296 | tf_op args[0]
  3.0 18.1 %share_rows.1 = (bf16[2,768,512]{2,1,0:T(8,128)(2,1)}, bf16[2,768,377]{2,1,0:T(8,128)(2,1)}) custom-call(bf16[768,393]{1,0:T(8,128)(2,1)} %copy.15.x_ref, bf16[768,377]{1,0:T(8,128)(2,1)} %t_ref.1), custom_call_target="tpu_custom_call" | custom-call | tf_op jit(solution)/shard_map/share_rows/pallas_call | solution.py:102
  21.1 0.0 copy-done.1
  21.2 0.0 copy-start.5
  21.2 0.0 copy-start.6
  21.2 4.2 %fusion.6 = bf16[1536,512]{1,0:T(8,128)(2,1)S(1)} fusion(bf16[1536,512]{1,0:T(8,128)(2,1)} %bitcast.31, s32[1536]{0:T(1024)S(1)} %reduce.2), kind=kOutput, calls=%fused_computation.12 | convolution fusion | flops 2419064832 | bytes 3151872 | tf_op jit(solution)/shard_map/dot_general | solution.py:258
  25.4 0.0 copy-done.5
  25.4 0.0 copy-done.6
  25.4 0.0 copy-start.2
  25.4 0.0 copy-start.3
  25.5 5.2 %multiply_convert_fusion = (bf16[1536,1024]{1,0:T(8,128)(2,1)}, f32[1536,1024]{1,0:T(8,128)}) fusion(f32[1024]{0:T(1024)S(1)} %bitcast.34, bf16[1536,512]{1,0:T(8,128)(2,1)S(1)} %fusion.6, bf16[393,1024]{1,0:T(8,128)(2,1)S(1)} %bitcast.33), kind=kOutput, calls=%fused_computation.4 | convolution fusion | flops 1620049920 | bytes 11819008 | tf_op jit(solution)/shard_map/dot_general | solution.py:262
  30.7 0.0 copy-done.2
  30.7 0.6 fusion.22
  31.3 0.0 copy-done.3
  31.3 0.0 copy-done
  31.3 0.0 copy-start.4
  31.3 0.0 slice-start
  31.3 3.9 %convolution_add_fusion = f32[1536,377]{1,0:T(8,128)S(1)} fusion(bf16[1536,1024]{1,0:T(8,128)(2,1)} %get-tuple-element.24, f32[377]{0:T(512)S(1)} %reduce.3, bf16[1,1024,377]{2,1,0:T(8,128)(2,1)S(1)} %copy-done), kind=kOutput, calls=%fused_computation.14 | convolution fusion | flops 1186518528 | bytes 6235620 | tf_op jit(solution)/shard_map/dot_general | solution.py:265
  35.2 0.0 copy-done.4
  35.2 0.0 slice-start.1
  35.2 4.2 %fusion.10 = (f32[]{:T(128)}, f32[377]{0:T(512)S(1)}, f32[377]{0:T(512)S(1)}, bf16[1536,377]{1,0:T(8,128)(2,1)S(1)}) fusion(f32[377]{0:T(512)S(1)} %get-tuple-element.20, f32[1536,377]{1,0:T(8,128)S(1)} %convolution_add_fusion, bf16[1536,377]{1,0:T(8,128)(2,1)S(1)} %bitcast.32, s32[1536]{0:T(1024)S(1)} %reduce.2), kind=kOutput, calls=%fused_computation.18 | convolution fusion | flops 1786479360 | bytes 4643248 | tf_op jit(solution)/shard_map/dot_general | solution.py:259
  39.4 0.0 slice-done
  39.4 0.0 slice-done.1
  39.4 3.9 %fusion.24 = (f32[1024]{0:T(1024)S(1)}, bf16[1536,1024]{1,0:T(8,128)(2,1)S(1)}) fusion(f32[1536,1024]{1,0:T(8,128)S(1)} %bitcast.37, f32[1024]{0:T(1024)S(1)} %bitcast.35, bf16[1536,377]{1,0:T(8,128)(2,1)S(1)} %get-tuple-element.21, bf16[1,1024,377]{2,1,0:T(8,128)(2,1)S(1)} %copy-done), kind=kOutput, calls=%fused_computation.37 | convolution fusion | flops 1203239936 | bytes 11375616 | tf_op jit(solution)/shard_map/dot_general | solution.py:275
  43.4 0.0 copy-start.7
  43.4 3.2 %fusion.11 = f32[1024,512]{1,0:T(8,128)} fusion(bf16[1536,512]{1,0:T(8,128)(2,1)S(1)} %fusion.6, bf16[1536,1024]{1,0:T(8,128)(2,1)S(1)} %get-tuple-element.27, f32[1024]{0:T(1024)S(1)} %get-tuple-element.26, pred[512]{0:T(512)(128)(4,1)S(1)} %iota_compare_fusion.7), kind=kOutput, calls=%fused_computation.19 | convolution fusion | flops 1611137024 | bytes 6820352 | tf_op jit(solution)/shard_map/dot_general | solution.py:243
  46.6 0.0 copy-done.7
  46.6 3.0 %fusion.14 = f32[1024,384]{1,0:T(8,128)} fusion(bf16[1536,1024]{1,0:T(8,128)(2,1)S(1)} %copy-done.7, bf16[1536,377]{1,0:T(8,128)(2,1)S(1)} %get-tuple-element.21), kind=kOutput, calls=%fused_computation.20 | convolution fusion | flops 1207959552 | bytes 5876736 | tf_op jit(solution)/shard_map/dot_general | solution.py:243
  50.9 0.1 pad.17.clone
  51.0 0.1 maximum_maximum_fusion
  51.0 0.6 pad.14.s_ref
  51.6 48.2 %reduce_grads.1 = (f32[64,512]{1,0:T(8,128)}, f32[64,384]{1,0:T(8,128)}, f32[8,384]{1,0:T(8,128)}) custom-call(f32[2,2,2,2,64,512]{5,4,3,2,1,0:T(8,128)} %bitcast.28, f32[2,2,2,2,64,384]{5,4,3,2,1,0:T(8,128)} %bitcast.29, f32[8,384]{1,0:T(8,128)} %pad.14.s_ref), custom_call_target="tpu_custom_call" | custom-call | tf_op jit(solution)/shard_map/reduce_grads/pallas_call | solution.py:216
  99.8 1.6 %slice_bitcast_fusion = f32[1,64,393]{2,1,0:T(8,128)} fusion(f32[64,512]{1,0:T(8,128)} %get-tuple-element.13), kind=kLoop, calls=%fused_computation.26 | loop fusion | bytes 201216 | tf_op jit(solution)/shard_map/broadcast_in_dim | solution.py:291
  101.4 1.5 %slice_reduce_fusion = f32[64]{0:T(128)} fusion(f32[64,512]{1,0:T(8,128)} %get-tuple-element.13), kind=kLoop, calls=%fused_computation.28 | loop fusion | bytes 512 | tf_op jit(solution)/shard_map/slice | solution.py:292
  102.8 1.5 %slice_bitcast_fusion.1 = f32[1,64,377]{2,1,0:T(8,128)} fusion(f32[64,384]{1,0:T(8,128)} %get-tuple-element.14), kind=kLoop, calls=%fused_computation.27 | loop fusion | bytes 193024 | tf_op jit(solution)/shard_map/broadcast_in_dim | solution.py:293
  104.4 1.4 %fusion.23 = (f32[1,377]{1,0:T(1,128)}, f32[1,377]{1,0:T(1,128)}) fusion(f32[8,384]{1,0:T(8,128)} %get-tuple-element.15), kind=kLoop, calls=%fused_computation.36 | loop fusion | bytes 6032 | tf_op jit(solution)/shard_map/slice | solution.py:295
  105.7 1.2 %slice.23 = f32[1,1]{1,0:T(1,128)} slice(f32[8,384]{1,0:T(8,128)} %get-tuple-element.15), slice={[2:3], [0:1]} | slice | bytes 8 | tf_op jit(solution)/shard_map/slice | solution.py:296
  (7 shorter events, 0.1 us)
Async XLA Ops:
  0.6 30.7 %copy-start = (bf16[1,1024,377]{2,1,0:T(8,128)(2,1)S(1)}, bf16[1,1024,377]{2,1,0:T(8,128)(2,1)}, u32[]{:S(2)}) copy-start(bf16[1,1024,377]{2,1,0:T(8,128)(2,1)} %param.13) | copy-start | bytes 2316292
  0.6 20.5 %copy-start.1 = (s32[1,1536]{1,0:T(1,128)S(1)}, s32[1,1536]{1,0:T(1,128)}, u32[]{:S(2)}) copy-start(s32[1,1536]{1,0:T(1,128)} %param.10) | copy-start | bytes 18436
  21.2 4.3 %copy-start.5 = (bf16[1,393,1024]{2,1,0:T(8,128)(2,1)S(1)}, bf16[1,393,1024]{2,1,0:T(8,128)(2,1)}, u32[]{:S(2)}) copy-start(bf16[1,393,1024]{2,1,0:T(8,128)(2,1)} %param.11) | copy-start | bytes 2414596
  21.2 4.3 %copy-start.6 = (f32[1,1024]{1,0:T(1,128)S(1)}, f32[1,1024]{1,0:T(1,128)}, u32[]{:S(2)}) copy-start(f32[1,1024]{1,0:T(1,128)} %param.12) | copy-start | bytes 12292
  25.4 5.2 %copy-start.2 = (f32[1,377]{1,0:T(1,128)S(1)}, f32[1,377]{1,0:T(1,128)}, u32[]{:S(2)}) copy-start(f32[1,377]{1,0:T(1,128)} %param.15) | copy-start | bytes 4528
  25.4 5.8 %copy-start.3 = (f32[1,377]{1,0:T(1,128)S(1)}, f32[1,377]{1,0:T(1,128)}, u32[]{:S(2)}) copy-start(f32[1,377]{1,0:T(1,128)} %param.14) | copy-start | bytes 4528
  31.3 3.9 %copy-start.4 = (bf16[2,768,377]{2,1,0:T(8,128)(2,1)S(1)}, bf16[2,768,377]{2,1,0:T(8,128)(2,1)}, u32[]{:S(2)}) copy-start(bf16[2,768,377]{2,1,0:T(8,128)(2,1)} %get-tuple-element.12) | copy-start | bytes 3474436
  31.3 8.1 %slice-start = ((s8[6291456]{0:T(1024)(128)(4,1)}), s8[4194304]{0:T(1024)(128)(4,1)S(1)}, s32[]{:S(2)}) async-start(s8[6291456]{0:T(1024)(128)(4,1)} %bitcast.36), calls=%async_computation | async-start | bytes 8388608
  35.2 4.2 %slice-start.1 = ((s8[6291456]{0:T(1024)(128)(4,1)}), s8[2097152]{0:T(1024)(128)(4,1)S(1)}, s32[]{:S(2)}) async-start(s8[6291456]{0:T(1024)(128)(4,1)} %bitcast.36), calls=%async_computation.1 | async-start | bytes 4194304
  43.4 3.2 %copy-start.7 = (bf16[1536,1024]{1,0:T(8,128)(2,1)S(1)}, bf16[1536,1024]{1,0:T(8,128)(2,1)}, u32[]{:S(2)}) copy-start(bf16[1536,1024]{1,0:T(8,128)(2,1)} %get-tuple-element.24) | copy-start | bytes 9437188

commit v2 on v1

--- a/solution.py
+++ b/solution.py
@@ -30,7 +30,7 @@
 
 def rows_kernel(
     n, m, x_ref, t_ref, rows_ref, goals_ref,
-    member_slots, dp_slots, member_sems, dp_sems, rows_sems, goal_sems,
+    held, member_slots, dp_slots, member_sems, dp_sems, rows_sems, goal_sems,
 ):
     d, c = lax.axis_index("dp"), lax.axis_index("member")
     count, width = x_ref.shape
@@ -59,6 +59,9 @@
         to_member(member_slots.at[c], member_slots.at[c], member_sems, o) for o in range(1, m)
     ]
     for copy in stat_copies:
+        copy.start()
+    row_copies = [to_member(x_ref, held.at[c], rows_sems, o) for o in range(1, m)]
+    for copy in row_copies:
         copy.start()
     goal_copies = [to_member(t_ref, goals_ref.at[c], goal_sems, o) for o in range(1, m)]
     for copy in goal_copies:
@@ -79,26 +82,28 @@
     for copy in dp_copies:
         copy.start()
     goals_ref[c] = t_ref[...]
+    held[c] = x_ref[...]
     edge = width // LANES * LANES
     if rows_ref.shape[2] > width:
-        rows_ref[c, :, edge:] = jnp.zeros((count, rows_ref.shape[2] - edge), rows_ref.dtype)
+        rows_ref[:, :, edge:] = jnp.zeros((m, count, rows_ref.shape[2] - edge), rows_ref.dtype)
+    for copy in row_copies:
+        copy.wait()
     for copy in dp_copies:
         copy.wait()
     total, spread = merge_stats(dp_slots, n, width, count * m)
     mean = total / (count * m * n)
     scale = 1.0 / jnp.sqrt(spread / (count * m * n) + 1e-06)
-    rows_ref[c, :, 0:width] = ((x_ref[...].astype(jnp.float32) - mean) * scale).astype(jnp.bfloat16)
-    row_copies = [to_member(rows_ref.at[c], rows_ref.at[c], rows_sems, o) for o in range(1, m)]
-    for copy in row_copies:
-        copy.start()
-    for copy in goal_copies + row_copies:
+    for i in range(m):
+        values = held[i].astype(jnp.float32)
+        rows_ref[i, :, 0:width] = ((values - mean) * scale).astype(jnp.bfloat16)
+    for copy in goal_copies:
         copy.wait()
 
 
 def shared_rows(n, m, inputs, targets):
     count, width = inputs.shape
     goal_width = targets.shape[1]
-    wide = pad_lanes(width)
+    wide = pad_lanes(width + 1)
     rows, goals = pl.pallas_call(
         functools.partial(rows_kernel, n, m),
         out_shape=(
@@ -108,6 +113,7 @@
         in_specs=[pl.BlockSpec(memory_space=pltpu.VMEM)] * 2,
         out_specs=(pl.BlockSpec(memory_space=pltpu.VMEM),) * 2,
         scratch_shapes=[
+            pltpu.VMEM((m, count, width), inputs.dtype),
             pltpu.VMEM((m, 8, wide), jnp.float32),
             pltpu.VMEM((n, 8, wide), jnp.float32),
             pltpu.SemaphoreType.DMA((2, m)),

time: 107 us -> 105 us (0.981)
  Pallas kernels: 66.3 us -> 64.2 us
    pallas_call x1, Pallas kernels: 18.1 us -> 16.4 us  [shared_rows(): pl.pallas_call(functools.partial(rows_kernel, n, m), out_shape=(jax.Shape...]
where the time goes in v2:
time: 105 us
  Pallas kernels  64.2 us (61%)
  matrix products  27.6 us (26%)
  local copies, waits for them, and re-layouts  10.2 us (10%)
  between operations  2.11 us (2%)
    pallas_call x1, Pallas kernels, reduce_grads(): pl.pallas_call(functools.partial(grads_kernel, n, bits, plan), out_shape=...  47.8 us
    pallas_call x1, Pallas kernels, shared_rows(): pl.pallas_call(functools.partial(rows_kernel, n, m), out_shape=(jax.Shape...  16.4 us
    dot_general x2, matrix products, outer_rows(): lax.dot_general(left, right, (((0,), (0,)), ((), ())), preferred_element_...  6.19 us
    dot_general x1, matrix products, per_device(): jnp.dot(picked, weight_wide, preferred_element_type=jnp.float32)  5.22 us
    dot_general x1, matrix products, per_device(): jnp.dot(choose, row_block, preferred_element_type=jnp.float32)  4.23 us
    dot_general x1, matrix products, per_device(): goal_rows = jnp.dot(choose, goal_block, preferred_element_type=jnp.float32)  4.21 us
    dot_general x1, matrix products, per_device(): lax.dot_general(grad_half, upper_weight, (((1,), (1,)), ((), ())), prefer...  3.9 us
    dot_general x1, matrix products, per_device(): jnp.dot(hidden, upper_weight, preferred_element_type=jnp.float32)  3.87 us

profile of v2, /device:TPU:0, one launch (start us, length us, event | category | flops | bytes accessed | tf_op | source)
XLA Modules:
  0.0 104.8 jit_solution(14252410399220955920)
XLA Ops:
  0.6 0.0 copy-start
  0.6 0.0 copy-start.1
  0.7 2.3 %copy.15.x_ref = bf16[768,393]{1,0:T(8,128)(2,1)} copy(bf16[768,393]{0,1:T(8,128)(2,1)} %param.8) | data formatting | bytes 1207296 | tf_op args[0]
  3.0 16.4 %share_rows.1 = (bf16[2,768,512]{2,1,0:T(8,128)(2,1)}, bf16[2,768,377]{2,1,0:T(8,128)(2,1)}) custom-call(bf16[768,393]{1,0:T(8,128)(2,1)} %copy.15.x_ref, bf16[768,377]{1,0:T(8,128)(2,1)} %t_ref.1), custom_call_target="tpu_custom_call" | custom-call | tf_op jit(solution)/shard_map/share_rows/pallas_call | solution.py:107
  19.4 0.0 copy-done.1
  19.4 0.0 copy-start.5
  19.4 0.0 copy-start.6
  19.5 4.2 %fusion.6 = bf16[1536,512]{1,0:T(8,128)(2,1)S(1)} fusion(bf16[1536,512]{1,0:T(8,128)(2,1)} %bitcast.31, s32[1536]{0:T(1024)S(1)} %reduce.2), kind=kOutput, calls=%fused_computation.12 | convolution fusion | flops 2419064832 | bytes 3151872 | tf_op jit(solution)/shard_map/dot_general | solution.py:264
  23.7 0.0 copy-done.5
  23.7 0.0 copy-done.6
  23.7 0.0 copy-start.2
  23.7 0.0 copy-start.3
  23.7 5.2 %multiply_convert_fusion = (bf16[1536,1024]{1,0:T(8,128)(2,1)}, f32[1536,1024]{1,0:T(8,128)}) fusion(f32[1024]{0:T(1024)S(1)} %bitcast.34, bf16[1536,512]{1,0:T(8,128)(2,1)S(1)} %fusion.6, bf16[393,1024]{1,0:T(8,128)(2,1)S(1)} %bitcast.33), kind=kOutput, calls=%fused_computation.4 | convolution fusion | flops 1620049920 | bytes 11819008 | tf_op jit(solution)/shard_map/dot_general | solution.py:268
  29.0 0.0 copy-done.2
  29.0 0.6 fusion.22
  29.6 0.0 copy-done.3
  29.6 0.0 copy-done
  29.6 0.0 copy-start.4
  29.6 0.0 slice-start
  29.6 3.9 %convolution_add_fusion = f32[1536,377]{1,0:T(8,128)S(1)} fusion(bf16[1536,1024]{1,0:T(8,128)(2,1)} %get-tuple-element.24, f32[377]{0:T(512)S(1)} %reduce.3, bf16[1,1024,377]{2,1,0:T(8,128)(2,1)S(1)} %copy-done), kind=kOutput, calls=%fused_computation.14 | convolution fusion | flops 1186518528 | bytes 6235620 | tf_op jit(solution)/shard_map/dot_general | solution.py:271
  33.5 0.0 copy-done.4
  33.5 0.0 slice-start.1
  33.5 4.2 %fusion.10 = (f32[]{:T(128)}, f32[377]{0:T(512)S(1)}, f32[377]{0:T(512)S(1)}, bf16[1536,377]{1,0:T(8,128)(2,1)S(1)}) fusion(f32[377]{0:T(512)S(1)} %get-tuple-element.20, f32[1536,377]{1,0:T(8,128)S(1)} %convolution_add_fusion, bf16[1536,377]{1,0:T(8,128)(2,1)S(1)} %bitcast.32, s32[1536]{0:T(1024)S(1)} %reduce.2), kind=kOutput, calls=%fused_computation.18 | convolution fusion | flops 1786479360 | bytes 4643248 | tf_op jit(solution)/shard_map/dot_general | solution.py:265
  37.7 0.0 slice-done
  37.7 0.0 slice-done.1
  37.7 3.9 %fusion.24 = (f32[1024]{0:T(1024)S(1)}, bf16[1536,1024]{1,0:T(8,128)(2,1)S(1)}) fusion(f32[1536,1024]{1,0:T(8,128)S(1)} %bitcast.37, f32[1024]{0:T(1024)S(1)} %bitcast.35, bf16[1536,377]{1,0:T(8,128)(2,1)S(1)} %get-tuple-element.21, bf16[1,1024,377]{2,1,0:T(8,128)(2,1)S(1)} %copy-done), kind=kOutput, calls=%fused_computation.37 | convolution fusion | flops 1203239936 | bytes 11375616 | tf_op jit(solution)/shard_map/dot_general | solution.py:281
  41.6 0.0 copy-start.7
  41.6 3.2 %fusion.11 = f32[1024,512]{1,0:T(8,128)} fusion(bf16[1536,512]{1,0:T(8,128)(2,1)S(1)} %fusion.6, bf16[1536,1024]{1,0:T(8,128)(2,1)S(1)} %get-tuple-element.27, f32[1024]{0:T(1024)S(1)} %get-tuple-element.26, pred[512]{0:T(512)(128)(4,1)S(1)} %iota_compare_fusion.7), kind=kOutput, calls=%fused_computation.19 | convolution fusion | flops 1611137024 | bytes 6820352 | tf_op jit(solution)/shard_map/dot_general | solution.py:249
  44.8 0.0 copy-done.7
  44.9 3.0 %fusion.14 = f32[1024,384]{1,0:T(8,128)} fusion(bf16[1536,1024]{1,0:T(8,128)(2,1)S(1)} %copy-done.7, bf16[1536,377]{1,0:T(8,128)(2,1)S(1)} %get-tuple-element.21), kind=kOutput, calls=%fused_computation.20 | convolution fusion | flops 1207959552 | bytes 5876736 | tf_op jit(solution)/shard_map/dot_general | solution.py:249
  49.2 0.1 pad.17.clone
  49.2 0.1 maximum_maximum_fusion
  49.3 0.6 pad.14.s_ref
  49.9 47.8 %reduce_grads.1 = (f32[64,512]{1,0:T(8,128)}, f32[64,384]{1,0:T(8,128)}, f32[8,384]{1,0:T(8,128)}) custom-call(f32[2,2,2,2,64,512]{5,4,3,2,1,0:T(8,128)} %bitcast.28, f32[2,2,2,2,64,384]{5,4,3,2,1,0:T(8,128)} %bitcast.29, f32[8,384]{1,0:T(8,128)} %pad.14.s_ref), custom_call_target="tpu_custom_call" | custom-call | tf_op jit(solution)/shard_map/reduce_grads/pallas_call | solution.py:222
  97.7 1.6 %slice_bitcast_fusion = f32[1,64,393]{2,1,0:T(8,128)} fusion(f32[64,512]{1,0:T(8,128)} %get-tuple-element.13), kind=kLoop, calls=%fused_computation.26 | loop fusion | bytes 201216 | tf_op jit(solution)/shard_map/broadcast_in_dim | solution.py:297
  99.3 1.5 %slice_reduce_fusion = f32[64]{0:T(128)} fusion(f32[64,512]{1,0:T(8,128)} %get-tuple-element.13), kind=kLoop, calls=%fused_computation.28 | loop fusion | bytes 512 | tf_op jit(solution)/shard_map/slice | solution.py:298
  100.7 1.5 %slice_bitcast_fusion.1 = f32[1,64,377]{2,1,0:T(8,128)} fusion(f32[64,384]{1,0:T(8,128)} %get-tuple-element.14), kind=kLoop, calls=%fused_computation.27 | loop fusion | bytes 193024 | tf_op jit(solution)/shard_map/broadcast_in_dim | solution.py:299
  102.2 1.4 %fusion.23 = (f32[1,377]{1,0:T(1,128)}, f32[1,377]{1,0:T(1,128)}) fusion(f32[8,384]{1,0:T(8,128)} %get-tuple-element.15), kind=kLoop, calls=%fused_computation.36 | loop fusion | bytes 6032 | tf_op jit(solution)/shard_map/slice | solution.py:301
  103.6 1.2 %slice.23 = f32[1,1]{1,0:T(1,128)} slice(f32[8,384]{1,0:T(8,128)} %get-tuple-element.15), slice={[2:3], [0:1]} | slice | bytes 8 | tf_op jit(solution)/shard_map/slice | solution.py:302
  (7 shorter events, 0.1 us)
Async XLA Ops:
  0.6 29.0 %copy-start = (bf16[1,1024,377]{2,1,0:T(8,128)(2,1)S(1)}, bf16[1,1024,377]{2,1,0:T(8,128)(2,1)}, u32[]{:S(2)}) copy-start(bf16[1,1024,377]{2,1,0:T(8,128)(2,1)} %param.13) | copy-start | bytes 2316292
  0.6 18.7 %copy-start.1 = (s32[1,1536]{1,0:T(1,128)S(1)}, s32[1,1536]{1,0:T(1,128)}, u32[]{:S(2)}) copy-start(s32[1,1536]{1,0:T(1,128)} %param.10) | copy-start | bytes 18436
  19.4 4.3 %copy-start.5 = (bf16[1,393,1024]{2,1,0:T(8,128)(2,1)S(1)}, bf16[1,393,1024]{2,1,0:T(8,128)(2,1)}, u32[]{:S(2)}) copy-start(bf16[1,393,1024]{2,1,0:T(8,128)(2,1)} %param.11) | copy-start | bytes 2414596
  19.4 4.3 %copy-start.6 = (f32[1,1024]{1,0:T(1,128)S(1)}, f32[1,1024]{1,0:T(1,128)}, u32[]{:S(2)}) copy-start(f32[1,1024]{1,0:T(1,128)} %param.12) | copy-start | bytes 12292
  23.7 5.2 %copy-start.2 = (f32[1,377]{1,0:T(1,128)S(1)}, f32[1,377]{1,0:T(1,128)}, u32[]{:S(2)}) copy-start(f32[1,377]{1,0:T(1,128)} %param.15) | copy-start | bytes 4528
  23.7 5.8 %copy-start.3 = (f32[1,377]{1,0:T(1,128)S(1)}, f32[1,377]{1,0:T(1,128)}, u32[]{:S(2)}) copy-start(f32[1,377]{1,0:T(1,128)} %param.14) | copy-start | bytes 4528
  29.6 3.9 %copy-start.4 = (bf16[2,768,377]{2,1,0:T(8,128)(2,1)S(1)}, bf16[2,768,377]{2,1,0:T(8,128)(2,1)}, u32[]{:S(2)}) copy-start(bf16[2,768,377]{2,1,0:T(8,128)(2,1)} %get-tuple-element.12) | copy-start | bytes 3474436
  29.6 8.1 %slice-start = ((s8[6291456]{0:T(1024)(128)(4,1)}), s8[4194304]{0:T(1024)(128)(4,1)S(1)}, s32[]{:S(2)}) async-start(s8[6291456]{0:T(1024)(128)(4,1)} %bitcast.36), calls=%async_computation | async-start | bytes 8388608
  33.5 4.2 %slice-start.1 = ((s8[6291456]{0:T(1024)(128)(4,1)}), s8[2097152]{0:T(1024)(128)(4,1)S(1)}, s32[]{:S(2)}) async-start(s8[6291456]{0:T(1024)(128)(4,1)} %bitcast.36), calls=%async_computation.1 | async-start | bytes 4194304
  41.6 3.2 %copy-start.7 = (bf16[1536,1024]{1,0:T(8,128)(2,1)S(1)}, bf16[1536,1024]{1,0:T(8,128)(2,1)}, u32[]{:S(2)}) copy-start(bf16[1536,1024]{1,0:T(8,128)(2,1)} %get-tuple-element.24) | copy-start | bytes 9437188
